TPU v7x, 32 devices: a whole 2x2x4 slice. The times are simulated.
32 devices in a mesh: slab: 8 (over y, x, core), det: 4 (over z).
Axes of the slice: x: 2, y: 2, z: 4, core: 2. Of those that a mesh axis runs over, the one named last changes fastest.
Arguments:
- traces: float32 [32, 128, 4096], P(('slab', 'det')), may hold values from -6 to 6
- tables: bfloat16 [32, 256, 2048], P('slab', None, 'det'), may hold values from -0.0625 to 0.0625
- slab_range: int32 [32, 2], P(('slab', 'det')), may hold values from 0 to 7, as said below
- table_slot: int32 [32, 7], P(('slab', 'det')), may hold values from 0 to 3
- sample_start: int32 [32, 7], P(('slab', 'det')), may hold values from 0 to 3840
Outputs:
- image: float32 [128, 16384], P(None, ('slab', 'det'))
Inputs may be any that keep to these rules, and one draw needn't show every extreme that they name: For detector d with home slab g = d // 4: max(0, g - 3) <= slab_range[d, 0] <= g <= slab_range[d, 1] <= min(7, g + 3); some detectors reach the full 3 on both sides where the grid allows.
All inputs are finite; a program needn't handle non-finite values.
Results may differ from a plain program's by a relative error of at most 0.007.
Values may be sent and summed in bfloat16 or wider, within the bound.
No kernel may reach another device: no remote copies, remote signals or barrier semaphores. Data moves between devices by JAX's collectives and lax.ppermute only.
A program may use at most 64 MiB of HBM per device.

v0:
```python
import jax
import jax.numpy as jnp
from jax import lax
from jax.sharding import PartitionSpec as P

KWIN = 256
NTAB = 4
RANGE = 3


def shifted(x, axis, by):
    peers = lax.axis_size(axis)
    pairs = [(i, i + by) for i in range(peers) if 0 <= i + by < peers]
    return lax.ppermute(x, axis, pairs)


def cut_windows(trace_rows, starts):

    def single(trace_row, first_index):
        return lax.dynamic_slice_in_dim(trace_row, first_index, KWIN, 1)

    return jax.vmap(single)(trace_rows, starts)


def bin_windows(windows, slot_ids, active):
    onehot = (slot_ids[:, None] == jnp.arange(NTAB, dtype=jnp.int32)[None, :]) & active[:, None]
    onehot = onehot.astype(jnp.bfloat16)
    return jnp.einsum("it,ifk->tfk", onehot, windows, preferred_element_type=jnp.float32)


def body(traces, tables, slab_range, table_slot, sample_start):
    position = lax.axis_index("slab")
    samples = traces.astype(jnp.bfloat16)
    own_active = (slab_range[:, 0] <= position) & (position <= slab_range[:, 1])
    stacked = bin_windows(
        cut_windows(samples, sample_start[:, RANGE]), table_slot[:, RANGE], own_active
    )
    for offset in list(range(-RANGE, 0)) + list(range(1, RANGE + 1)):
        target = position + offset
        active = (slab_range[:, 0] <= target) & (target <= slab_range[:, 1])
        windows = cut_windows(samples, sample_start[:, offset + RANGE])
        windows = windows * active[:, None, None].astype(jnp.bfloat16)
        arrived_windows, arrived_slots = shifted(
            (windows, table_slot[:, offset + RANGE]), "slab", offset
        )
        everything = jnp.ones(arrived_slots.shape, jnp.bool_)
        stacked = stacked + bin_windows(arrived_windows, arrived_slots, everything)
    binned = stacked.astype(jnp.bfloat16)
    partial_image = jnp.einsum(
        "tfk,tkv->fv",
        binned,
        lax.all_gather(tables, "det", axis=2, tiled=True),
        preferred_element_type=jnp.float32,
    )
    return lax.psum_scatter(partial_image, "det", scatter_dimension=1, tiled=True)


def solution(mesh):
    placed = (
        P(("slab", "det"), None, None),
        P("slab", None, "det"),
        P(("slab", "det"), None),
        P(("slab", "det"), None),
        P(("slab", "det"), None),
    )
    return jax.shard_map(
        body, mesh=mesh, in_specs=placed, out_specs=P(None, ("slab", "det")), check_vma=False
    )
```

profile of v0, /device:TPU:0, one launch (start us, length us, event | category | flops | bytes accessed | tf_op | source)
XLA Modules:
  0.0 129.3 jit_solution(1520195266104620349)
XLA Ops:
  6.5 0.7 all-gather.2.cloned.1.call-update
  7.3 1.6 %fusion.21 = (s32[1,1]{1,0:T(1,128)}, s32[1,1]{1,0:T(1,128)}, s32[1,1]{1,0:T(1,128)}, s32[1,1]{1,0:T(1,128)}, s32[1,1]{1,0:T(1,128)}, /*index=5*/s32[1,1]{1,0:T(1,128)}, s32[1,1]{1,0:T(1,128)}) fusion(s32[1,7]{1,0:T(1,128)} %param.8), kind=kLoop, calls=%fused_computation.43 | loop fusion | bytes 56 | tf_op jit(solution)/shard_map/slice | solution.py:36
  8.9 3.0 %collective-permute-start.6 = (s32[1]{0:T(128)}, s32[1]{0:T(128)}, u32[]{:S(2)}, u32[]{:S(2)}) collective-permute-start(s32[1]{0:T(128)} %bitcast.33), channel_id=1, source_target_pairs={{0,4},{4,8},{8,12},{12,16},{16,20},{20,24},{24,28},{1,5},{5,9},{9,... | collective-permute-start | bytes 20 | tf_op jit(solution)/shard_map/ppermute | solution.py:14
  11.9 1.3 collective-permute-start.4
  13.1 1.3 collective-permute-start.2
  14.4 1.3 collective-permute-start
  15.7 7.7 %collective-permute-start.10 = (s32[1]{0:T(128)}, s32[1]{0:T(128)}, u32[]{:S(2)}, u32[]{:S(2)}) collective-permute-start(s32[1]{0:T(128)} %bitcast.49), channel_id=1, source_target_pairs={{0,12},{4,16},{8,20},{12,24},{16,28},{1,13},{5,17},{9,21},{13,25},... | collective-permute-start | bytes 20 | tf_op jit(solution)/shard_map/ppermute | solution.py:14
  23.4 1.3 %fusion.23 = (s32[1,1]{1,0:T(1,128)}, s32[1,1]{1,0:T(1,128)}) fusion(s32[1,2]{1,0:T(1,128)} %param.7), kind=kLoop, calls=%fused_computation.45 | loop fusion | bytes 16 | tf_op jit(solution)/shard_map/slice | solution.py:34
  33.7 1.6 %fusion.22 = (s32[1,1]{1,0:T(1,128)}, s32[1,1]{1,0:T(1,128)}, s32[1,1]{1,0:T(1,128)}, s32[1,1]{1,0:T(1,128)}, s32[1,1]{1,0:T(1,128)}, /*index=5*/s32[1,1]{1,0:T(1,128)}, s32[1,1]{1,0:T(1,128)}) fusion(s32[1,7]{1,0:T(1,128)} %param.9), kind=kLoop, calls=%fused_computation.44 | loop fusion | bytes 56 | tf_op jit(solution)/shard_map/slice | solution.py:36
  44.2 1.7 %convert_element_type.10 = bf16[1,128,4096]{2,1,0:T(8,128)(2,1)S(1)} convert(f32[1,128,4096]{2,1,0:T(8,128)} %param.5) | non-fusion elementwise | flops 524288 | bytes 3145728 | tf_op jit(solution)/shard_map/convert_element_type | solution.py:33
  51.2 5.9 %collective-permute-start.8 = (s32[1]{0:T(128)}, s32[1]{0:T(128)}, u32[]{:S(2)}, u32[]{:S(2)}) collective-permute-start(s32[1]{0:T(128)} %bitcast.41), channel_id=1, source_target_pairs={{0,8},{4,12},{8,16},{12,20},{16,24},{20,28},{1,9},{5,13},{9,17},{1... | collective-permute-start | bytes 20 | tf_op jit(solution)/shard_map/ppermute | solution.py:14
  57.1 0.7 fusion.18
  57.8 1.3 %collective-permute-start.11 = (bf16[1,128,256]{2,1,0:T(8,128)(2,1)S(1)}, bf16[1,128,256]{2,1,0:T(8,128)(2,1)S(1)}, u32[]{:S(2)}, u32[]{:S(2)}) collective-permute-start(bf16[1,128,256]{2,1,0:T(8,128)(2,1)S(1)} %get-tuple-element.83), channel_id=1, source_target_pairs={{0,12},{4,16},{8,20},{12,24},{16,28},{1,13},{5,17},{9,21},{13,25},... | collective-permute-start | bytes 196616 | tf_op jit(solution)/shard_map/ppermute | solution.py:14
  59.8 2.9 %collective-permute-start.9 = (bf16[1,128,256]{2,1,0:T(8,128)(2,1)S(1)}, bf16[1,128,256]{2,1,0:T(8,128)(2,1)S(1)}, u32[]{:S(2)}, u32[]{:S(2)}) collective-permute-start(bf16[1,128,256]{2,1,0:T(8,128)(2,1)S(1)} %get-tuple-element.84), channel_id=1, source_target_pairs={{0,8},{4,12},{8,16},{12,20},{16,24},{20,28},{1,9},{5,13},{9,17},{1... | collective-permute-start | bytes 196616 | tf_op jit(solution)/shard_map/ppermute | solution.py:14
  63.3 1.3 %collective-permute-start.7 = (bf16[1,128,256]{2,1,0:T(8,128)(2,1)S(1)}, bf16[1,128,256]{2,1,0:T(8,128)(2,1)S(1)}, u32[]{:S(2)}, u32[]{:S(2)}) collective-permute-start(bf16[1,128,256]{2,1,0:T(8,128)(2,1)S(1)} %get-tuple-element.85), channel_id=1, source_target_pairs={{0,4},{4,8},{8,12},{12,16},{16,20},{20,24},{24,28},{1,5},{5,9},{9,... | collective-permute-start | bytes 196616 | tf_op jit(solution)/shard_map/ppermute | solution.py:14
  65.3 1.3 collective-permute-start.5
  67.2 1.3 collective-permute-start.3
  68.5 0.7 fusion.19
  69.2 1.3 collective-permute-start.1
  70.6 4.5 %collective-permute-done.3 = bf16[1,128,256]{2,1,0:T(8,128)(2,1)S(1)} collective-permute-done((bf16[1,128,256]{2,1,0:T(8,128)(2,1)S(1)}, bf16[1,128,256]{2,1,0:T(8,128)(2,1)S(1)}, u32[]{:S(2)}, u32[]{:S(2)}) %collective-permute-start.3) | collective-permute-done | bytes 65568 | tf_op jit(solution)/shard_map/ppermute | solution.py:14
  75.1 1.9 %collective-permute-done.1 = bf16[1,128,256]{2,1,0:T(8,128)(2,1)S(1)} collective-permute-done((bf16[1,128,256]{2,1,0:T(8,128)(2,1)S(1)}, bf16[1,128,256]{2,1,0:T(8,128)(2,1)S(1)}, u32[]{:S(2)}, u32[]{:S(2)}) %collective-permute-start.1) | collective-permute-done | bytes 65568 | tf_op jit(solution)/shard_map/ppermute | solution.py:14
  77.0 15.4 %all-gather.2.cloned.1.call-done = bf16[4,256,2048]{2,1,0:T(8,128)(2,1)} async-done(((bf16[4,256,512]{2,1,0:T(8,128)(2,1)}), bf16[4,256,2048]{2,1,0:T(8,128)(2,1)}) %all-gather.2.cloned.1.call-update) | async-done | bytes 4194320 | tf_op jit(solution)/shard_map/all_gather | solution.py:52
  92.4 4.1 %convolution_bitcast_fusion = f32[128,2048]{1,0:T(8,128)} fusion(bf16[4,256,2048]{2,1,0:T(8,128)(2,1)} %all-gather.2.cloned.1.call-done, f32[128,256]{1,0:T(8,128)S(1)} %bitcast_convert_fusion, f32[4]{0:T(128)S(1)} %fusion.20, f32[128,256]{1,0:T(8,128)S(1)} %bitcast_convert_fusion.1, f32[4]{0:T(128)S(1)} %fusion.19, f32[128,256]{1,0:T(8,128)S(1)} %bitcast_convert_fusion.2, ...), kind=kOutput, calls=%fused_computation | convolution fusion | flops 538705920 | bytes 6160496 | tf_op jit(solution)/shard_map/tfk,tkv->fv/dot_general | solution.py:49
  96.5 25.9 %reduce-scatter.2.cloned.1.call-done = f32[128,512]{1,0:T(8,128)} async-done(((f32[128,2048]{1,0:T(8,128)}), f32[128,512]{1,0:T(8,128)}) %reduce-scatter.2.cloned.1.call-update) | async-done | bytes 262160 | tf_op jit(solution)/shard_map/reduce_scatter | solution.py:55
  (25 shorter events, 3.5 us)
Async XLA Ops:
  6.5 85.9 %all-gather.2.cloned.1.call-start = ((), (), s32[]{:S(2)}) async-start(), calls=%async_computation.1 | async-start | bytes 5242880 | tf_op jit(solution)/shard_map/all_gather | solution.py:52
  7.3 115.2 %reduce-scatter.2.cloned.1.call-start = ((), (), s32[]{:S(2)}) async-start(), calls=%async_computation.2 | async-start | bytes 1310720 | tf_op jit(solution)/shard_map/reduce_scatter | solution.py:55
  8.9 42.3 %collective-permute-start.6 = (s32[1]{0:T(128)}, s32[1]{0:T(128)}, u32[]{:S(2)}, u32[]{:S(2)}) collective-permute-start(s32[1]{0:T(128)} %bitcast.33), channel_id=1, source_target_pairs={{0,4},{4,8},{8,12},{12,16},{16,20},{20,24},{24,28},{1,5},{5,9},{9,... | collective-permute-start | bytes 20 | tf_op jit(solution)/shard_map/ppermute | solution.py:14
  11.9 46.0 %collective-permute-start.4 = (s32[1]{0:T(128)}, s32[1]{0:T(128)}, u32[]{:S(2)}, u32[]{:S(2)}) collective-permute-start(s32[1]{0:T(128)} %bitcast.25), channel_id=1, source_target_pairs={{4,0},{8,4},{12,8},{16,12},{20,16},{24,20},{28,24},{5,1},{9,5},{13... | collective-permute-start | bytes 20 | tf_op jit(solution)/shard_map/ppermute | solution.py:14
  13.1 46.6 %collective-permute-start.2 = (s32[1]{0:T(128)}, s32[1]{0:T(128)}, u32[]{:S(2)}, u32[]{:S(2)}) collective-permute-start(s32[1]{0:T(128)} %bitcast.17), channel_id=1, source_target_pairs={{8,0},{12,4},{16,8},{20,12},{24,16},{28,20},{9,1},{13,5},{17,9},{2... | collective-permute-start | bytes 20 | tf_op jit(solution)/shard_map/ppermute | solution.py:14
  14.4 48.8 %collective-permute-start = (s32[1]{0:T(128)}, s32[1]{0:T(128)}, u32[]{:S(2)}, u32[]{:S(2)}) collective-permute-start(s32[1]{0:T(128)} %bitcast.9), channel_id=1, source_target_pairs={{12,0},{16,4},{20,8},{24,12},{28,16},{13,1},{17,5},{21,9},{25,13},... | collective-permute-start | bytes 20 | tf_op jit(solution)/shard_map/ppermute | solution.py:14
  15.7 49.5 %collective-permute-start.10 = (s32[1]{0:T(128)}, s32[1]{0:T(128)}, u32[]{:S(2)}, u32[]{:S(2)}) collective-permute-start(s32[1]{0:T(128)} %bitcast.49), channel_id=1, source_target_pairs={{0,12},{4,16},{8,20},{12,24},{16,28},{1,13},{5,17},{9,21},{13,25},... | collective-permute-start | bytes 20 | tf_op jit(solution)/shard_map/ppermute | solution.py:14
  51.2 16.0 %collective-permute-start.8 = (s32[1]{0:T(128)}, s32[1]{0:T(128)}, u32[]{:S(2)}, u32[]{:S(2)}) collective-permute-start(s32[1]{0:T(128)} %bitcast.41), channel_id=1, source_target_pairs={{0,8},{4,12},{8,16},{12,20},{16,24},{20,28},{1,9},{5,13},{9,17},{1... | collective-permute-start | bytes 20 | tf_op jit(solution)/shard_map/ppermute | solution.py:14
  57.8 11.4 %collective-permute-start.11 = (bf16[1,128,256]{2,1,0:T(8,128)(2,1)S(1)}, bf16[1,128,256]{2,1,0:T(8,128)(2,1)S(1)}, u32[]{:S(2)}, u32[]{:S(2)}) collective-permute-start(bf16[1,128,256]{2,1,0:T(8,128)(2,1)S(1)} %get-tuple-element.83), channel_id=1, source_target_pairs={{0,12},{4,16},{8,20},{12,24},{16,28},{1,13},{5,17},{9,21},{13,25},... | collective-permute-start | bytes 196616 | tf_op jit(solution)/shard_map/ppermute | solution.py:14
  59.8 10.7 %collective-permute-start.9 = (bf16[1,128,256]{2,1,0:T(8,128)(2,1)S(1)}, bf16[1,128,256]{2,1,0:T(8,128)(2,1)S(1)}, u32[]{:S(2)}, u32[]{:S(2)}) collective-permute-start(bf16[1,128,256]{2,1,0:T(8,128)(2,1)S(1)} %get-tuple-element.84), channel_id=1, source_target_pairs={{0,8},{4,12},{8,16},{12,20},{16,24},{20,28},{1,9},{5,13},{9,17},{1... | collective-permute-start | bytes 196616 | tf_op jit(solution)/shard_map/ppermute | solution.py:14
  63.3 7.2 %collective-permute-start.7 = (bf16[1,128,256]{2,1,0:T(8,128)(2,1)S(1)}, bf16[1,128,256]{2,1,0:T(8,128)(2,1)S(1)}, u32[]{:S(2)}, u32[]{:S(2)}) collective-permute-start(bf16[1,128,256]{2,1,0:T(8,128)(2,1)S(1)} %get-tuple-element.85), channel_id=1, source_target_pairs={{0,4},{4,8},{8,12},{12,16},{16,20},{20,24},{24,28},{1,5},{5,9},{9,... | collective-permute-start | bytes 196616 | tf_op jit(solution)/shard_map/ppermute | solution.py:14
  65.3 5.3 %collective-permute-start.5 = (bf16[1,128,256]{2,1,0:T(8,128)(2,1)S(1)}, bf16[1,128,256]{2,1,0:T(8,128)(2,1)S(1)}, u32[]{:S(2)}, u32[]{:S(2)}) collective-permute-start(bf16[1,128,256]{2,1,0:T(8,128)(2,1)S(1)} %get-tuple-element.86), channel_id=1, source_target_pairs={{4,0},{8,4},{12,8},{16,12},{20,16},{24,20},{28,24},{5,1},{9,5},{13... | collective-permute-start | bytes 196616 | tf_op jit(solution)/shard_map/ppermute | solution.py:14
  67.2 7.9 %collective-permute-start.3 = (bf16[1,128,256]{2,1,0:T(8,128)(2,1)S(1)}, bf16[1,128,256]{2,1,0:T(8,128)(2,1)S(1)}, u32[]{:S(2)}, u32[]{:S(2)}) collective-permute-start(bf16[1,128,256]{2,1,0:T(8,128)(2,1)S(1)} %get-tuple-element.87), channel_id=1, source_target_pairs={{8,0},{12,4},{16,8},{20,12},{24,16},{28,20},{9,1},{13,5},{17,9},{2... | collective-permute-start | bytes 196616 | tf_op jit(solution)/shard_map/ppermute | solution.py:14
  69.2 7.8 %collective-permute-start.1 = (bf16[1,128,256]{2,1,0:T(8,128)(2,1)S(1)}, bf16[1,128,256]{2,1,0:T(8,128)(2,1)S(1)}, u32[]{:S(2)}, u32[]{:S(2)}) collective-permute-start(bf16[1,128,256]{2,1,0:T(8,128)(2,1)S(1)} %get-tuple-element.88), channel_id=1, source_target_pairs={{12,0},{16,4},{20,8},{24,12},{28,16},{13,1},{17,5},{21,9},{25,13},... | collective-permute-start | bytes 196616 | tf_op jit(solution)/shard_map/ppermute | solution.py:14
Sparse Core Ops, SparseCore 0:
  8.9 83.4 all-gather.1
  96.6 25.7 reduce-scatter.1
where the time goes:
time: 130 us; the launch traced here: 129 us
  waiting for transfers between devices  48.5 us (37%)
  between operations  36 us (28%)
  starting transfers between devices  29.8 us (23%)
  other arithmetic  6.48 us (5%)
  local copies, waits for them, and re-layouts  4.5 us (3%)
  matrix products  4.07 us (3%)
    ppermute x12, starting transfers between devices, shifted(): return lax.ppermute(x, axis, pairs)  29.8 us
    reduce_scatter x1, waiting for transfers between devices, body(): lax.psum_scatter(partial_image, 'det', scatter_dimension=1, tiled=True)  25.9 us
    all_gather x1, waiting for transfers between devices, body(): lax.all_gather(tables, 'det', axis=2, tiled=True)  15.4 us
    ppermute x12, waiting for transfers between devices, shifted(): return lax.ppermute(x, axis, pairs)  6.42 us
    another operation x14, other arithmetic  4.75 us
    dot_general x1, matrix products, body(): jnp.einsum('tfk,tkv->fv', binned, lax.all_gather(tables, 'det', axis=2, t...  4.07 us
  transfers between devices with their start and end apart: 14, of which 4 were waited for; matrix products, arithmetic and copies ran while one was open for 8% of the time, Pallas kernels for 0%

commit v1 on v0

--- a/solution.py
+++ b/solution.py
@@ -1,3 +1,4 @@
+import functools
 import jax
 import jax.numpy as jnp
 from jax import lax
@@ -6,6 +7,14 @@
 KWIN = 256
 NTAB = 4
 RANGE = 3
+
+
+def limits_answer(xs, ax_name):
+    finding = jax.lax.all_gather(xs, ax_name)
+    return jnp.concatenate(finding, axis=2)
+
+
+press_tracks = functools.partial(limits_answer, ax_name="det")
 
 
 def shifted(x, axis, by):
@@ -47,10 +56,7 @@
         stacked = stacked + bin_windows(arrived_windows, arrived_slots, everything)
     binned = stacked.astype(jnp.bfloat16)
     partial_image = jnp.einsum(
-        "tfk,tkv->fv",
-        binned,
-        lax.all_gather(tables, "det", axis=2, tiled=True),
-        preferred_element_type=jnp.float32,
+        "tfk,tkv->fv", binned, press_tracks(tables), preferred_element_type=jnp.float32
     )
     return lax.psum_scatter(partial_image, "det", scatter_dimension=1, tiled=True)
 

time: 130 us -> 145 us (1.12)
  local copies, waits for them, and re-layouts: 4.5 us -> 18.8 us
  waiting for transfers between devices: 48.5 us -> 53.3 us
  starting transfers between devices: 29.8 us -> 25.2 us
    ppermute x12, waiting for transfers between devices: 6.42 us -> 15.6 us  [shifted(): return lax.ppermute(x, axis, pairs)]
    reshape x0 -> x1, local copies, waits for them, and re-layouts: none -> 7.73 us  [limits_answer(): return jnp.concatenate(finding, axis=2)]
    all_gather x0 -> x1, local copies, waits for them, and re-layouts: none -> 7.4 us  [limits_answer(): finding = jax.lax.all_gather(xs, ax_name)]
    ppermute x12, starting transfers between devices: 29.8 us -> 25.2 us  [shifted(): return lax.ppermute(x, axis, pairs)]
    all_gather x1, waiting for transfers between devices: 15.4 us -> 11 us  [limits_answer(): finding = jax.lax.all_gather(xs, ax_name)]
  transfers between devices with their start and end apart: 14 -> 14, of which waited for: 4 -> 7; matrix products, arithmetic and copies ran while one was open for 8% -> 7% of each run, Pallas kernels for 0% -> 0%
where the time goes in v1:
time: 145 us; the launch traced here: 144 us
  waiting for transfers between devices  53.3 us (37%)
  between operations  36.5 us (25%)
  starting transfers between devices  25.2 us (17%)
  local copies, waits for them, and re-layouts  18.8 us (13%)
  other arithmetic  6.5 us (4%)
  matrix products  4.08 us (3%)
    reduce_scatter x1, waiting for transfers between devices, body(): lax.psum_scatter(partial_image, 'det', scatter_dimension=1, tiled=True)  25.9 us
    ppermute x12, starting transfers between devices, shifted(): return lax.ppermute(x, axis, pairs)  25.2 us
    ppermute x12, waiting for transfers between devices, shifted(): return lax.ppermute(x, axis, pairs)  15.6 us
    all_gather x1, waiting for transfers between devices, limits_answer(): finding = jax.lax.all_gather(xs, ax_name)  11 us
    reshape x1, local copies, waits for them, and re-layouts, limits_answer(): return jnp.concatenate(finding, axis=2)  7.73 us
    all_gather x1, local copies, waits for them, and re-layouts, limits_answer(): finding = jax.lax.all_gather(xs, ax_name)  7.4 us
    another operation x14, other arithmetic  4.76 us
    dot_general x1, matrix products, body(): jnp.einsum('tfk,tkv->fv', binned, press_tracks(tables), preferred_element...  4.08 us
  transfers between devices with their start and end apart: 14, of which 7 were waited for; matrix products, arithmetic and copies ran while one was open for 7% of the time, Pallas kernels for 0%

profile of v1, /device:TPU:0, one launch (start us, length us, event | category | flops | bytes accessed | tf_op | source)
XLA Modules:
  0.0 144.4 jit_solution(2626503096963585066)
XLA Ops:
  7.3 1.6 %fusion.22 = (s32[1,1]{1,0:T(1,128)}, s32[1,1]{1,0:T(1,128)}, s32[1,1]{1,0:T(1,128)}, s32[1,1]{1,0:T(1,128)}, s32[1,1]{1,0:T(1,128)}, /*index=5*/s32[1,1]{1,0:T(1,128)}, s32[1,1]{1,0:T(1,128)}) fusion(s32[1,7]{1,0:T(1,128)} %param.9), kind=kLoop, calls=%fused_computation.45 | loop fusion | bytes 56 | tf_op jit(solution)/shard_map/slice | solution.py:45
  11.5 1.4 fusion.23
  27.3 1.7 %convert_element_type.10 = bf16[1,128,4096]{2,1,0:T(8,128)(2,1)S(1)} convert(f32[1,128,4096]{2,1,0:T(8,128)} %param.5) | non-fusion elementwise | flops 524288 | bytes 3145728 | tf_op jit(solution)/shard_map/convert_element_type | solution.py:42
  33.7 4.3 %collective-permute-start.11 = (bf16[1,128,256]{2,1,0:T(8,128)(2,1)S(1)}, bf16[1,128,256]{2,1,0:T(8,128)(2,1)S(1)}, u32[]{:S(2)}, u32[]{:S(2)}) collective-permute-start(bf16[1,128,256]{2,1,0:T(8,128)(2,1)S(1)} %get-tuple-element.83), channel_id=1, source_target_pairs={{0,12},{4,16},{8,20},{12,24},{16,28},{1,13},{5,17},{9,21},{13,25},... | collective-permute-start | bytes 196616 | tf_op jit(solution)/shard_map/ppermute | solution.py:23
  38.7 4.2 %collective-permute-start.10 = (s32[1]{0:T(128)}, s32[1]{0:T(128)}, u32[]{:S(2)}, u32[]{:S(2)}) collective-permute-start(s32[1]{0:T(128)} %bitcast.49), channel_id=1, source_target_pairs={{0,12},{4,16},{8,20},{12,24},{16,28},{1,13},{5,17},{9,21},{13,25},... | collective-permute-start | bytes 20 | tf_op jit(solution)/shard_map/ppermute | solution.py:23
  42.9 1.3 collective-permute-start.9
  44.2 3.8 %collective-permute-start.8 = (s32[1]{0:T(128)}, s32[1]{0:T(128)}, u32[]{:S(2)}, u32[]{:S(2)}) collective-permute-start(s32[1]{0:T(128)} %bitcast.41), channel_id=1, source_target_pairs={{0,8},{4,12},{8,16},{12,20},{16,24},{20,28},{1,9},{5,13},{9,17},{1... | collective-permute-start | bytes 20 | tf_op jit(solution)/shard_map/ppermute | solution.py:23
  48.0 1.3 collective-permute-start.7
  51.4 2.6 %collective-permute-start.6 = (s32[1]{0:T(128)}, s32[1]{0:T(128)}, u32[]{:S(2)}, u32[]{:S(2)}) collective-permute-start(s32[1]{0:T(128)} %bitcast.33), channel_id=1, source_target_pairs={{0,4},{4,8},{8,12},{12,16},{16,20},{20,24},{24,28},{1,5},{5,9},{9,... | collective-permute-start | bytes 20 | tf_op jit(solution)/shard_map/ppermute | solution.py:23
  54.6 1.3 collective-permute-start.5
  56.6 1.3 collective-permute-start.4
  58.5 1.9 %collective-permute-done.4 = s32[1]{0:T(128)} collective-permute-done((s32[1]{0:T(128)}, s32[1]{0:T(128)}, u32[]{:S(2)}, u32[]{:S(2)}) %collective-permute-start.4) | collective-permute-done | bytes 36 | tf_op jit(solution)/shard_map/ppermute | solution.py:23
  60.4 1.3 collective-permute-start.2
  62.4 4.0 %collective-permute-done.2 = s32[1]{0:T(128)} collective-permute-done((s32[1]{0:T(128)}, s32[1]{0:T(128)}, u32[]{:S(2)}, u32[]{:S(2)}) %collective-permute-start.2) | collective-permute-done | bytes 36 | tf_op jit(solution)/shard_map/ppermute | solution.py:23
  66.3 1.3 collective-permute-start
  68.2 3.9 %collective-permute-done = s32[1]{0:T(128)} collective-permute-done((s32[1]{0:T(128)}, s32[1]{0:T(128)}, u32[]{:S(2)}, u32[]{:S(2)}) %collective-permute-start) | collective-permute-done | bytes 36 | tf_op jit(solution)/shard_map/ppermute | solution.py:23
  74.1 1.3 collective-permute-start.1
  75.5 3.9 %collective-permute-done.3 = bf16[1,128,256]{2,1,0:T(8,128)(2,1)S(1)} collective-permute-done((bf16[1,128,256]{2,1,0:T(8,128)(2,1)S(1)}, bf16[1,128,256]{2,1,0:T(8,128)(2,1)S(1)}, u32[]{:S(2)}, u32[]{:S(2)}) %collective-permute-start.3) | collective-permute-done | bytes 65568 | tf_op jit(solution)/shard_map/ppermute | solution.py:23
  79.5 1.9 %collective-permute-done.1 = bf16[1,128,256]{2,1,0:T(8,128)(2,1)S(1)} collective-permute-done((bf16[1,128,256]{2,1,0:T(8,128)(2,1)S(1)}, bf16[1,128,256]{2,1,0:T(8,128)(2,1)S(1)}, u32[]{:S(2)}, u32[]{:S(2)}) %collective-permute-start.1) | collective-permute-done | bytes 65568 | tf_op jit(solution)/shard_map/ppermute | solution.py:23
  81.4 11.0 %all-gather.3.cloned.1.call-done = bf16[16,256,512]{2,1,0:T(8,128)(2,1)} async-done(((bf16[4,256,512]{2,1,0:T(8,128)(2,1)}), bf16[16,256,512]{2,1,0:T(8,128)(2,1)}) %all-gather.3.cloned.1.call-update) | async-done | bytes 4194320 | tf_op jit(solution)/shard_map/all_gather | solution.py:13
  92.4 7.4 %copy.9 = bf16[4,4,256,512]{3,0,2,1:T(4,128)(2,1)} copy(bf16[4,4,256,512]{3,2,1,0:T(8,128)(2,1)} %bitcast.86) | data formatting | bytes 8388608 | tf_op jit(solution)/shard_map/all_gather | solution.py:13
  99.8 7.7 %reshape.308 = bf16[4,256,2048]{2,1,0:T(8,128)(2,1)} reshape(bf16[4,256,4,512]{3,2,1,0:T(4,128)(2,1)} %bitcast.85) | data formatting | bytes 8388608 | tf_op jit(solution)/shard_map/reshape | solution.py:14
  107.5 4.1 %convolution_bitcast_fusion = f32[128,2048]{1,0:T(8,128)} fusion(bf16[4,256,2048]{2,1,0:T(8,128)(2,1)} %reshape.308, f32[128,256]{1,0:T(8,128)S(1)} %bitcast_convert_fusion, f32[4]{0:T(128)S(1)} %fusion.20, f32[128,256]{1,0:T(8,128)S(1)} %bitcast_convert_fusion.1, f32[4]{0:T(128)S(1)} %fusion.19, f32[128,256]{1,0:T(8,128)S(1)} %bitcast_convert_fusion.2, ...), kind=kOutput, calls=%fused_computation.1 | convolution fusion | flops 538705920 | bytes 6160496 | tf_op jit(solution)/shard_map/tfk,tkv->fv/dot_general | solution.py:58
  111.6 25.9 %reduce-scatter.2.cloned.1.call-done = f32[128,512]{1,0:T(8,128)} async-done(((f32[128,2048]{1,0:T(8,128)}), f32[128,512]{1,0:T(8,128)}) %reduce-scatter.2.cloned.1.call-update) | async-done | bytes 262160 | tf_op jit(solution)/shard_map/reduce_scatter | solution.py:61
  (29 shorter events, 7.5 us)
Async XLA Ops:
  6.5 31.5 %copy-start = (s32[1,7]{1,0:T(1,128)S(1)}, s32[1,7]{1,0:T(1,128)}, u32[]{:S(2)}) copy-start(s32[1,7]{1,0:T(1,128)} %param.8) | copy-start | bytes 88
  6.5 85.9 %all-gather.3.cloned.1.call-start = ((), (), s32[]{:S(2)}) async-start(), calls=%async_computation.2 | async-start | bytes 5242880 | tf_op jit(solution)/shard_map/all_gather | solution.py:13
  7.3 130.3 %reduce-scatter.2.cloned.1.call-start = ((), (), s32[]{:S(2)}) async-start(), calls=%async_computation.1 | async-start | bytes 1310720 | tf_op jit(solution)/shard_map/reduce_scatter | solution.py:61
  33.7 40.4 %collective-permute-start.11 = (bf16[1,128,256]{2,1,0:T(8,128)(2,1)S(1)}, bf16[1,128,256]{2,1,0:T(8,128)(2,1)S(1)}, u32[]{:S(2)}, u32[]{:S(2)}) collective-permute-start(bf16[1,128,256]{2,1,0:T(8,128)(2,1)S(1)} %get-tuple-element.83), channel_id=1, source_target_pairs={{0,12},{4,16},{8,20},{12,24},{16,28},{1,13},{5,17},{9,21},{13,25},... | collective-permute-start | bytes 196616 | tf_op jit(solution)/shard_map/ppermute | solution.py:23
  38.7 12.6 %collective-permute-start.10 = (s32[1]{0:T(128)}, s32[1]{0:T(128)}, u32[]{:S(2)}, u32[]{:S(2)}) collective-permute-start(s32[1]{0:T(128)} %bitcast.49), channel_id=1, source_target_pairs={{0,12},{4,16},{8,20},{12,24},{16,28},{1,13},{5,17},{9,21},{13,25},... | collective-permute-start | bytes 20 | tf_op jit(solution)/shard_map/ppermute | solution.py:23
  42.9 32.5 %collective-permute-start.9 = (bf16[1,128,256]{2,1,0:T(8,128)(2,1)S(1)}, bf16[1,128,256]{2,1,0:T(8,128)(2,1)S(1)}, u32[]{:S(2)}, u32[]{:S(2)}) collective-permute-start(bf16[1,128,256]{2,1,0:T(8,128)(2,1)S(1)} %get-tuple-element.84), channel_id=1, source_target_pairs={{0,8},{4,12},{8,16},{12,20},{16,24},{20,28},{1,9},{5,13},{9,17},{1... | collective-permute-start | bytes 196616 | tf_op jit(solution)/shard_map/ppermute | solution.py:23
  44.2 10.3 %collective-permute-start.8 = (s32[1]{0:T(128)}, s32[1]{0:T(128)}, u32[]{:S(2)}, u32[]{:S(2)}) collective-permute-start(s32[1]{0:T(128)} %bitcast.41), channel_id=1, source_target_pairs={{0,8},{4,12},{8,16},{12,20},{16,24},{20,28},{1,9},{5,13},{9,17},{1... | collective-permute-start | bytes 20 | tf_op jit(solution)/shard_map/ppermute | solution.py:23
  48.0 27.5 %collective-permute-start.7 = (bf16[1,128,256]{2,1,0:T(8,128)(2,1)S(1)}, bf16[1,128,256]{2,1,0:T(8,128)(2,1)S(1)}, u32[]{:S(2)}, u32[]{:S(2)}) collective-permute-start(bf16[1,128,256]{2,1,0:T(8,128)(2,1)S(1)} %get-tuple-element.85), channel_id=1, source_target_pairs={{0,4},{4,8},{8,12},{12,16},{16,20},{20,24},{24,28},{1,5},{5,9},{9,... | collective-permute-start | bytes 196616 | tf_op jit(solution)/shard_map/ppermute | solution.py:23
  51.4 5.2 %collective-permute-start.6 = (s32[1]{0:T(128)}, s32[1]{0:T(128)}, u32[]{:S(2)}, u32[]{:S(2)}) collective-permute-start(s32[1]{0:T(128)} %bitcast.33), channel_id=1, source_target_pairs={{0,4},{4,8},{8,12},{12,16},{16,20},{20,24},{24,28},{1,5},{5,9},{9,... | collective-permute-start | bytes 20 | tf_op jit(solution)/shard_map/ppermute | solution.py:23
  54.6 21.0 %collective-permute-start.5 = (bf16[1,128,256]{2,1,0:T(8,128)(2,1)S(1)}, bf16[1,128,256]{2,1,0:T(8,128)(2,1)S(1)}, u32[]{:S(2)}, u32[]{:S(2)}) collective-permute-start(bf16[1,128,256]{2,1,0:T(8,128)(2,1)S(1)} %get-tuple-element.86), channel_id=1, source_target_pairs={{4,0},{8,4},{12,8},{16,12},{20,16},{24,20},{28,24},{5,1},{9,5},{13... | collective-permute-start | bytes 196616 | tf_op jit(solution)/shard_map/ppermute | solution.py:23
  56.6 3.9 %collective-permute-start.4 = (s32[1]{0:T(128)}, s32[1]{0:T(128)}, u32[]{:S(2)}, u32[]{:S(2)}) collective-permute-start(s32[1]{0:T(128)} %bitcast.25), channel_id=1, source_target_pairs={{4,0},{8,4},{12,8},{16,12},{20,16},{24,20},{28,24},{5,1},{9,5},{13... | collective-permute-start | bytes 20 | tf_op jit(solution)/shard_map/ppermute | solution.py:23
  60.4 5.9 %collective-permute-start.2 = (s32[1]{0:T(128)}, s32[1]{0:T(128)}, u32[]{:S(2)}, u32[]{:S(2)}) collective-permute-start(s32[1]{0:T(128)} %bitcast.17), channel_id=1, source_target_pairs={{8,0},{12,4},{16,8},{20,12},{24,16},{28,20},{9,1},{13,5},{17,9},{2... | collective-permute-start | bytes 20 | tf_op jit(solution)/shard_map/ppermute | solution.py:23
  66.3 5.8 %collective-permute-start = (s32[1]{0:T(128)}, s32[1]{0:T(128)}, u32[]{:S(2)}, u32[]{:S(2)}) collective-permute-start(s32[1]{0:T(128)} %bitcast.9), channel_id=1, source_target_pairs={{12,0},{16,4},{20,8},{24,12},{28,16},{13,1},{17,5},{21,9},{25,13},... | collective-permute-start | bytes 20 | tf_op jit(solution)/shard_map/ppermute | solution.py:23
  72.2 7.3 %collective-permute-start.3 = (bf16[1,128,256]{2,1,0:T(8,128)(2,1)S(1)}, bf16[1,128,256]{2,1,0:T(8,128)(2,1)S(1)}, u32[]{:S(2)}, u32[]{:S(2)}) collective-permute-start(bf16[1,128,256]{2,1,0:T(8,128)(2,1)S(1)} %get-tuple-element.87), channel_id=1, source_target_pairs={{8,0},{12,4},{16,8},{20,12},{24,16},{28,20},{9,1},{13,5},{17,9},{2... | collective-permute-start | bytes 196616 | tf_op jit(solution)/shard_map/ppermute | solution.py:23
  74.1 7.3 %collective-permute-start.1 = (bf16[1,128,256]{2,1,0:T(8,128)(2,1)S(1)}, bf16[1,128,256]{2,1,0:T(8,128)(2,1)S(1)}, u32[]{:S(2)}, u32[]{:S(2)}) collective-permute-start(bf16[1,128,256]{2,1,0:T(8,128)(2,1)S(1)} %get-tuple-element.88), channel_id=1, source_target_pairs={{12,0},{16,4},{20,8},{24,12},{28,16},{13,1},{17,5},{21,9},{25,13},... | collective-permute-start | bytes 196616 | tf_op jit(solution)/shard_map/ppermute | solution.py:23
Sparse Core Ops, SparseCore 0:
  8.9 83.4 all-gather.2
  111.8 25.7 reduce-scatter.1
